TPU v7x, 256 devices: a whole 4x4x8 slice. The times are simulated.
256 devices in a mesh: gx: 8 (over z), gy: 2 (over core), gz: 16 (over y, x).
Axes of the slice: x: 4, y: 4, z: 8, core: 2. Of those that a mesh axis runs over, the one named last changes fastest.
Arguments:
- pair: bfloat16 [128, 1024, 1024], P('gz', 'gx', 'gy'), may hold values from -6 to 6
- pair_mask: int32 [1024, 1024], P('gx', 'gy'), may hold values from 0 to 1, as said below
- input_gain: float32 [128], replicated, may hold values from 0.1 to 1.9
- input_weights: bfloat16 [4, 128, 128], replicated, may hold values from -0.5 to 0.5
- out_gate_weight: bfloat16 [128, 128], replicated, may hold values from -0.5 to 0.5
- hidden_gain: float32 [128], replicated, may hold values from 0.1 to 1.9
- out_weight: bfloat16 [128, 128], replicated, may hold values from -0.5 to 0.5
Outputs:
- update: bfloat16 [128, 1024, 1024], P('gz', 'gx', 'gy')
Inputs may be any that keep to these rules, and one draw needn't show every extreme that they name: pair_mask[r, s] = m[r] * m[s] for a 0/1 residue mask m of the draw that is 0 for all r >= L, for one crop length L with 512 < L <= 1024; residues below L may also be 0.
All inputs are finite; a program needn't handle non-finite values.
Results may differ from a plain program's by a relative error of at most 0.011.
Values may be sent and summed in bfloat16 or wider, within the bound.
A program may use at most 64 MiB of HBM per device.

v0:
```python
import jax
import jax.numpy as jnp
from jax import lax
from jax.sharding import PartitionSpec as P

EPSILON = 1e-05


def layer_norm(values, gains):
    average = jnp.mean(values, axis=0)
    spread = jnp.mean(jnp.square(values - average), axis=0)
    normed = (values - average) * lax.rsqrt(spread + EPSILON) * gains[:, None, None]
    return normed.astype(jnp.bfloat16)


def exchange(value, axis, split_dim, concat_dim):
    return lax.all_to_all(value, axis, split_axis=split_dim, concat_axis=concat_dim, tiled=True)


def shards(pair, pair_mask, input_gain, input_weights, out_gate_weight, hidden_gain, out_weight):
    channels = input_gain.shape[0]
    hidden = hidden_gain.shape[0]
    rows = pair.shape[1] // lax.axis_size("gz")
    share_mask = lax.dynamic_slice_in_dim(pair_mask, lax.axis_index("gz") * rows, rows, 0).astype(
        jnp.float32
    )
    normed = layer_norm(exchange(pair, "gz", 1, 0).astype(jnp.float32), input_gain)
    weights = jnp.concatenate([*input_weights, out_gate_weight], axis=1)
    product = jnp.einsum("dk,drs->krs", weights, normed, preferred_element_type=jnp.float32)
    left_gate, left, right_gate, right = (product[k * hidden : (k + 1) * hidden] for k in range(4))
    gate = share_mask * jax.nn.sigmoid(product[4 * hidden :])
    sides = jnp.stack(
        [
            (share_mask * jax.nn.sigmoid(left_gate) * left).astype(jnp.bfloat16),
            (share_mask * jax.nn.sigmoid(right_gate) * right).astype(jnp.bfloat16),
        ],
        axis=1,
    )
    sides = exchange(sides, "gz", 0, 2)
    sides = exchange(sides, "gx", 0, 2)
    left_side = lax.all_gather(sides[:, 0], "gy", axis=2, tiled=True)
    triangle = jnp.einsum(
        "hki,hkj->hij", left_side, sides[:, 1], preferred_element_type=jnp.float32
    ).astype(jnp.bfloat16)
    triangle = exchange(triangle, "gx", 1, 0)
    triangle = exchange(triangle, "gz", 1, 0)
    hidden_normed = layer_norm(triangle.astype(jnp.float32), hidden_gain)
    projected = jnp.einsum(
        "hc,hij->cij", out_weight, hidden_normed, preferred_element_type=jnp.float32
    )
    update = (gate * projected).astype(jnp.bfloat16)
    return exchange(update, "gz", 0, 1)


def solution(mesh):
    placed = (P("gz", "gx", "gy"), P("gx", "gy"), P(), P(), P(), P(), P())
    return jax.shard_map(
        shards, mesh=mesh, in_specs=placed, out_specs=P("gz", "gx", "gy"), check_vma=False
    )
```

profile of v0, /device:TPU:2, one launch (start us, length us, event | category | flops | bytes accessed | tf_op | source)
XLA Modules:
  0.0 246.9 jit_solution(13325242700693101154)
XLA Ops:
  6.5 0.0 copy-start
  6.5 2.8 %copy.62 = bf16[8,128,512]{2,0,1:T(8,128)(2,1)} copy(bf16[8,128,512]{2,1,0:T(8,128)(2,1)} %param.7) | data formatting | bytes 2097152 | tf_op args[0]
  9.4 7.5 %all-to-all-start = ((bf16[8,128,512]{2,0,1:T(8,128)(2,1)}), bf16[8,128,512]{2,0,1:T(8,128)(2,1)S(1)}, u32[]{:S(2)}, u32[]{:S(2)}) async-start(bf16[8,128,512]{2,0,1:T(8,128)(2,1)} %copy.62), calls=%async_computation | async-start | bytes 2097152 | tf_op jit(solution)/shard_map/all_to_all | solution.py:17
  16.8 0.0 all-gather.3.cloned.1.call-start
  16.9 0.0 copy-done.2
  16.9 0.1 copy.77
  17.0 0.1 copy.78
  17.2 0.1 copy.79
  17.3 0.1 copy.80
  17.4 0.0 copy-done.3
  17.4 0.1 copy.61
  17.5 0.7 dynamic-slice_convert_fusion
  18.3 14.3 %all-to-all-done = bf16[8,128,512]{2,0,1:T(8,128)(2,1)S(1)} async-done(((bf16[8,128,512]{2,0,1:T(8,128)(2,1)}), bf16[8,128,512]{2,0,1:T(8,128)(2,1)S(1)}, u32[]{:S(2)}, u32[]{:S(2)}) %all-to-all-start) | async-done | bytes 1048608 | tf_op jit(solution)/shard_map/all_to_all | solution.py:17
  32.6 0.2 fusion.32
  32.8 0.3 multiply_reduce_fusion.1
  33.1 1.6 fusion.30
  34.8 1.4 fusion.38
  36.1 2.6 %copy-done.1 = f32[640,8,512]{2,0,1:T(8,128)} copy-done((f32[640,8,512]{2,0,1:T(8,128)}, f32[640,8,512]{2,0,1:T(8,128)S(1)}, u32[]{:S(2)}) %copy-start.1) | copy-done | bytes 10485784
  38.7 0.2 pad_maximum_fusion
  38.9 1.2 copy.64
  40.1 31.3 %all_to_all.84 = bf16[128,2,8,512]{3,2,1,0:T(8,128)(2,1)S(1)} all-to-all(bf16[128,2,8,512]{3,2,1,0:T(8,128)(2,1)S(1)} %copy.64), channel_id=1, replica_groups=mesh['gx'=8,'gy'=2,'gz'=16] {'gz'}, dimensions={0} | all-to-all | bytes 4194304 | tf_op jit(solution)/shard_map/all_to_all | solution.py:17
  71.4 0.2 copy.91
  71.6 58.1 %all_to_all.85 = bf16[8,2,128,512]{3,2,1,0:T(8,128)(2,1)S(1)} all-to-all(bf16[8,2,128,512]{3,2,1,0:T(8,128)(2,1)S(1)} %bitcast.101), channel_id=1, replica_groups=mesh['gx'=8,'gy'=2,'gz'=16] {'gx'}, dimensions={0} | all-to-all | bytes 4194304 | tf_op jit(solution)/shard_map/all_to_all | solution.py:17
  129.7 0.2 copy.66
  129.9 1.0 slice.33
  131.0 0.0 all-gather.3.cloned.1.call-update
  131.0 9.7 %all-gather.3.cloned.1.call-done = bf16[1,1,1024,1024]{3,2,1,0:T(8,128)(2,1)} async-done(((bf16[1,1,1024,512]{3,2,1,0:T(8,128)(2,1)}), bf16[1,1,1024,1024]{3,2,1,0:T(8,128)(2,1)}) %all-gather.3.cloned.1.call-update) | async-done | bytes 2097168 | tf_op jit(solution)/shard_map/all_gather | solution.py:41
  140.7 2.9 %fusion.27 = bf16[1,1024,512]{2,1,0:T(8,128)(2,1)S(1)} fusion(bf16[1,1,1024,1024]{3,2,1,0:T(8,128)(2,1)} %all-gather.3.cloned.1.call-done, bf16[1,2,1024,512]{3,2,1,0:T(8,128)(2,1)S(1)} %bitcast.104), kind=kOutput, calls=%fused_computation.38 | convolution fusion | flops 1074266112 | bytes 4194304 | tf_op jit(solution)/shard_map/hki,hkj->hij/dot_general | solution.py:42
  143.6 1.6 copy.93
  145.2 0.5 broadcast.58
  145.7 7.0 %reduce.4 = bf16[1024,512]{1,0:T(8,128)(2,1)S(1)} reduce(bf16[1024,1,512]{2,1,0:T(2,128)(2,1)S(1)} %bitcast.99, bf16[]{:T(256)} %broadcast.58), dimensions={1}, to_apply=%bitcast.95.reduce_sub_computation | reduce | bytes 2097154
  152.8 0.8 reshape.55
  153.6 36.0 %all_to_all.86 = bf16[8,2,32768]{2,1,0:T(2,128)(2,1)S(1)} all-to-all(bf16[8,2,32768]{2,1,0:T(2,128)(2,1)S(1)} %reshape.55), channel_id=1, replica_groups=mesh['gx'=8,'gy'=2,'gz'=16] {'gx'}, dimensions={0} | all-to-all | bytes 2097152 | tf_op jit(solution)/shard_map/all_to_all | solution.py:17
  189.6 1.0 reshape.56
  190.6 0.3 copy.76
  190.9 0.6 copy.68
  191.5 22.9 %all_to_all.87 = bf16[8,128,512]{2,0,1:T(8,128)(2,1)S(1)} all-to-all(bf16[8,128,512]{2,0,1:T(8,128)(2,1)S(1)} %copy.68), channel_id=1, replica_groups=mesh['gx'=8,'gy'=2,'gz'=16] {'gz'}, dimensions={1} | all-to-all | bytes 2097152 | tf_op jit(solution)/shard_map/all_to_all | solution.py:17
  214.4 0.3 fusion.33
  214.7 0.4 multiply_reduce_fusion
  215.1 0.3 convert_bitcast_fusion
  215.5 0.0 copy-start.5
  215.5 0.2 copy.70
  215.7 0.4 copy-done.5
  216.1 0.3 fusion.17
  216.4 2.5 %fusion.23 = bf16[128,8,512]{2,0,1:T(8,128)(2,1)S(1)} fusion(f32[640,8,512]{2,0,1:T(8,128)} %copy-done.1, bf16[128,8,512]{2,1,0:T(8,128)(2,1)S(1)} %fusion.17, f32[8,512]{1,0:T(8,128)S(1)} %dynamic-slice_convert_fusion, bf16[128,128]{1,0:T(8,128)(2,1)S(1)} %copy-done), kind=kOutput, calls=%fused_computation.36 | convolution fusion | flops 137363456 | bytes 4243456 | tf_op jit(solution)/shard_map/hc,hij->cij/dot_general | solution.py:48
  219.0 0.6 copy.73
  219.6 19.4 %all_to_all.88 = bf16[128,8,512]{2,1,0:T(8,128)(2,1)S(1)} all-to-all(bf16[128,8,512]{2,1,0:T(8,128)(2,1)S(1)} %copy.73), channel_id=1, replica_groups=mesh['gx'=8,'gy'=2,'gz'=16] {'gz'}, dimensions={0} | all-to-all | bytes 2097152 | tf_op jit(solution)/shard_map/all_to_all | solution.py:17
  239.0 1.1 copy.92
  (16 shorter events, 0.1 us)
Async XLA Ops:
  6.5 209.9 %copy-start = (bf16[128,128]{1,0:T(8,128)(2,1)S(1)}, bf16[128,128]{1,0:T(8,128)(2,1)}, u32[]{:S(2)}) copy-start(bf16[128,128]{1,0:T(8,128)(2,1)} %param.13) | copy-start | bytes 98308
  6.5 10.4 %copy-start.2 = (bf16[4,128,128]{2,1,0:T(8,128)(2,1)S(1)}, bf16[4,128,128]{2,1,0:T(8,128)(2,1)}, u32[]{:S(2)}) copy-start(bf16[4,128,128]{2,1,0:T(8,128)(2,1)} %param.10) | copy-start | bytes 393220
  6.5 10.9 %copy-start.3 = (bf16[128,128]{1,0:T(8,128)(2,1)S(1)}, bf16[128,128]{1,0:T(8,128)(2,1)}, u32[]{:S(2)}) copy-start(bf16[128,128]{1,0:T(8,128)(2,1)} %param.11) | copy-start | bytes 98308
  9.4 23.3 %all-to-all-start = ((bf16[8,128,512]{2,0,1:T(8,128)(2,1)}), bf16[8,128,512]{2,0,1:T(8,128)(2,1)S(1)}, u32[]{:S(2)}, u32[]{:S(2)}) async-start(bf16[8,128,512]{2,0,1:T(8,128)(2,1)} %copy.62), calls=%async_computation | async-start | bytes 2097152 | tf_op jit(solution)/shard_map/all_to_all | solution.py:17
  16.8 16.3 %copy-start.4 = (f32[128]{0:T(128)S(1)}, f32[128]{0:T(128)}, u32[]{:S(2)}) copy-start(f32[128]{0:T(128)} %param.9) | copy-start | bytes 1540
  16.8 123.9 %all-gather.3.cloned.1.call-start = ((), (), s32[]{:S(2)}) async-start(), calls=%async_computation.6 | async-start | bytes 3145728 | tf_op jit(solution)/shard_map/all_gather | solution.py:41
  34.8 4.0 %copy-start.1 = (f32[640,8,512]{2,0,1:T(8,128)}, f32[640,8,512]{2,0,1:T(8,128)S(1)}, u32[]{:S(2)}) copy-start(f32[640,8,512]{2,0,1:T(8,128)S(1)} %fusion.30) | copy-start | bytes 31457284
  215.5 0.7 copy-start.5
Sparse Core Ops, SparseCore 0:
  131.1 9.5 all-gather.2
where the time goes:
time: 247 us
  blocking collectives  168 us (68%)
  waiting for transfers between devices  24 us (10%)
  local copies, waits for them, and re-layouts  15.8 us (6%)
  between operations  13.7 us (6%)
  other arithmetic  11.2 us (5%)
  starting transfers between devices  7.52 us (3%)
  matrix products  7.01 us (3%)
    all_to_all x5, blocking collectives, exchange(): lax.all_to_all(value, axis, split_axis=split_dim, concat_axis=concat_dim,...  168 us
    all_to_all x1, waiting for transfers between devices, exchange(): lax.all_to_all(value, axis, split_axis=split_dim, concat_axis=concat_dim,...  14.3 us
    all_gather x1, waiting for transfers between devices, shards(): left_side = lax.all_gather(sides[:, 0], 'gy', axis=2, tiled=True)  9.71 us
    unnamed x26, local copies, waits for them, and re-layouts  9.09 us
    all_to_all x1, starting transfers between devices, exchange(): lax.all_to_all(value, axis, split_axis=split_dim, concat_axis=concat_dim,...  7.48 us
    unnamed x1, other arithmetic  7.04 us
  transfers between devices with their start and end apart: 2, of which 2 were waited for; matrix products, arithmetic and copies ran while one was open for 1% of the time, Pallas kernels for 0%

commit v1 on v0

--- a/solution.py
+++ b/solution.py
@@ -38,7 +38,11 @@
     )
     sides = exchange(sides, "gz", 0, 2)
     sides = exchange(sides, "gx", 0, 2)
-    left_side = lax.all_gather(sides[:, 0], "gy", axis=2, tiled=True)
+    x = sides[:, 0]
+    devices = lax.axis_size("gy")
+    blocks = jnp.stack([x for _ in range(devices)])
+    blocks = lax.all_to_all(blocks, "gy", split_axis=0, concat_axis=0)
+    left_side = jnp.concatenate(blocks, axis=2)
     triangle = jnp.einsum(
         "hki,hkj->hij", left_side, sides[:, 1], preferred_element_type=jnp.float32
     ).astype(jnp.bfloat16)

time: 247 us -> 226 us (0.915)
  between operations: 13.7 us -> 0.29 us
  waiting for transfers between devices: 24 us -> 14.3 us
  local copies, waits for them, and re-layouts: 15.8 us -> 18.3 us
    all_gather x1 -> x0, waiting for transfers between devices: 9.71 us -> none  [shards(): left_side = lax.all_gather(sides[:, 0], 'gy', axis=2, tiled=True)]
    all_to_all x5, blocking collectives: 168 us -> 161 us  [exchange(): lax.all_to_all(value, axis, split_axis=split_dim, concat_axis=concat_dim,...]
    all_to_all x0 -> x1, blocking collectives: none -> 5.41 us  [shards(): blocks = lax.all_to_all(blocks, 'gy', split_axis=0, concat_axis=0)]
    unnamed x26 -> x28, local copies, waits for them, and re-layouts: 9.09 us -> 10.2 us
  transfers between devices with their start and end apart: 2 -> 1, of which waited for: 2 -> 1; matrix products, arithmetic and copies ran while one was open for 1% -> 1% of each run, Pallas kernels for 0% -> 0%
where the time goes in v1:
time: 226 us
  blocking collectives  167 us (74%)
  local copies, waits for them, and re-layouts  18.3 us (8%)
  waiting for transfers between devices  14.3 us (6%)
  other arithmetic  11.4 us (5%)
  starting transfers between devices  7.48 us (3%)
  matrix products  7.24 us (3%)
    all_to_all x5, blocking collectives, exchange(): lax.all_to_all(value, axis, split_axis=split_dim, concat_axis=concat_dim,...  161 us
    all_to_all x1, waiting for transfers between devices, exchange(): lax.all_to_all(value, axis, split_axis=split_dim, concat_axis=concat_dim,...  14.3 us
    unnamed x28, local copies, waits for them, and re-layouts  10.2 us
    all_to_all x1, starting transfers between devices, exchange(): lax.all_to_all(value, axis, split_axis=split_dim, concat_axis=concat_dim,...  7.48 us
    unnamed x1, other arithmetic  7.04 us
    all_to_all x1, blocking collectives, shards(): blocks = lax.all_to_all(blocks, 'gy', split_axis=0, concat_axis=0)  5.41 us
  transfers between devices with their start and end apart: 1, of which 1 were waited for; matrix products, arithmetic and copies ran while one was open for 1% of the time, Pallas kernels for 0%

profile of v1, /device:TPU:2, one launch (start us, length us, event | category | flops | bytes accessed | tf_op | source)
XLA Modules:
  0.0 225.8 jit_solution(10772842726552245791)
XLA Ops:
  0.0 0.0 copy-start
  0.0 2.8 %copy.65 = bf16[8,128,512]{2,0,1:T(8,128)(2,1)} copy(bf16[8,128,512]{2,1,0:T(8,128)(2,1)} %param.7) | data formatting | bytes 2097152 | tf_op args[0]
  2.8 7.5 %all-to-all-start = ((bf16[8,128,512]{2,0,1:T(8,128)(2,1)}), bf16[8,128,512]{2,0,1:T(8,128)(2,1)S(1)}, u32[]{:S(2)}, u32[]{:S(2)}) async-start(bf16[8,128,512]{2,0,1:T(8,128)(2,1)} %copy.65), calls=%async_computation | async-start | bytes 2097152 | tf_op jit(solution)/shard_map/all_to_all | solution.py:17
  10.3 0.0 copy-done.3
  10.3 0.1 copy.81
  10.5 0.1 copy.82
  10.6 0.1 copy.83
  10.7 0.1 copy.84
  10.8 0.1 copy.64
  11.0 0.7 dynamic-slice_convert_fusion
  11.8 14.3 %all-to-all-done = bf16[8,128,512]{2,0,1:T(8,128)(2,1)S(1)} async-done(((bf16[8,128,512]{2,0,1:T(8,128)(2,1)}), bf16[8,128,512]{2,0,1:T(8,128)(2,1)S(1)}, u32[]{:S(2)}, u32[]{:S(2)}) %all-to-all-start) | async-done | bytes 1048608 | tf_op jit(solution)/shard_map/all_to_all | solution.py:17
  26.1 0.2 fusion.25
  26.3 0.3 multiply_reduce_fusion.1
  26.6 1.6 fusion.23
  28.2 1.4 fusion.31
  29.6 2.6 %copy-done.1 = f32[640,8,512]{2,0,1:T(8,128)} copy-done((f32[640,8,512]{2,0,1:T(8,128)}, f32[640,8,512]{2,0,1:T(8,128)S(1)}, u32[]{:S(2)}) %copy-start.1) | copy-done | bytes 10485784
  32.2 0.2 pad_maximum_fusion
  32.4 1.2 copy.67
  33.6 31.3 %all_to_all.89 = bf16[128,2,8,512]{3,2,1,0:T(8,128)(2,1)S(1)} all-to-all(bf16[128,2,8,512]{3,2,1,0:T(8,128)(2,1)S(1)} %copy.67), channel_id=1, replica_groups=mesh['gx'=8,'gy'=2,'gz'=16] {'gz'}, dimensions={0} | all-to-all | bytes 4194304 | tf_op jit(solution)/shard_map/all_to_all | solution.py:17
  64.9 0.2 copy.95
  65.1 58.1 %all_to_all.90 = bf16[8,2,128,512]{3,2,1,0:T(8,128)(2,1)S(1)} all-to-all(bf16[8,2,128,512]{3,2,1,0:T(8,128)(2,1)S(1)} %bitcast.97), channel_id=1, replica_groups=mesh['gx'=8,'gy'=2,'gz'=16] {'gx'}, dimensions={0} | all-to-all | bytes 4194304 | tf_op jit(solution)/shard_map/all_to_all | solution.py:17
  123.2 0.2 copy.69
  123.4 0.1 slice.33
  123.5 0.2 pad_maximum_fusion.1
  123.6 1.1 copy-done.2
  124.7 5.4 %all_to_all.91 = bf16[2,1,1024,512]{3,2,1,0:T(8,128)(2,1)S(1)} all-to-all(bf16[2,1,1024,512]{3,2,1,0:T(8,128)(2,1)S(1)} %pad_maximum_fusion.1), channel_id=1, replica_groups=mesh['gx'=8,'gy'=2,'gz'=16] {'gy'}, dimensions={0} | all-to-all | bytes 4194304 | tf_op jit(solution)/shard_map/all_to_all | solution.py:44
  130.1 2.4 %copy.70 = bf16[1,1024,2,512]{1,3,2,0:T(8,128)(2,1)} copy(bf16[1,1024,2,512]{3,1,0,2:T(8,128)(2,1)S(1)} %bitcast.99) | data formatting | bytes 4194304 | tf_op jit(solution)/shard_map/reshape | solution.py:45
  132.5 3.1 %fusion.22 = bf16[1,1024,512]{2,1,0:T(8,128)(2,1)S(1)} fusion(bf16[1024,1024]{0,1:T(8,128)(2,1)} %bitcast.104, bf16[1,2,1024,512]{3,2,1,0:T(8,128)(2,1)} %bitcast.101), kind=kOutput, calls=%fused_computation.37 | convolution fusion | flops 1074266112 | bytes 4194304 | tf_op jit(solution)/shard_map/hki,hkj->hij/dot_general | solution.py:46
  135.6 1.6 copy.97
  137.3 0.5 broadcast.58
  137.8 7.0 %reduce.4 = bf16[1024,512]{1,0:T(8,128)(2,1)S(1)} reduce(bf16[1024,1,512]{2,1,0:T(2,128)(2,1)S(1)} %bitcast.95, bf16[]{:T(256)} %broadcast.58), dimensions={1}, to_apply=%bitcast.91.reduce_sub_computation | reduce | bytes 2097154
  144.8 0.8 reshape.59
  145.6 31.8 %all_to_all.92 = bf16[8,2,32768]{2,1,0:T(2,128)(2,1)S(1)} all-to-all(bf16[8,2,32768]{2,1,0:T(2,128)(2,1)S(1)} %reshape.59), channel_id=1, replica_groups=mesh['gx'=8,'gy'=2,'gz'=16] {'gx'}, dimensions={0} | all-to-all | bytes 2097152 | tf_op jit(solution)/shard_map/all_to_all | solution.py:17
  177.4 1.0 reshape.60
  178.5 0.3 copy.80
  178.8 0.6 copy.72
  179.3 20.6 %all_to_all.93 = bf16[8,128,512]{2,0,1:T(8,128)(2,1)S(1)} all-to-all(bf16[8,128,512]{2,0,1:T(8,128)(2,1)S(1)} %copy.72), channel_id=1, replica_groups=mesh['gx'=8,'gy'=2,'gz'=16] {'gz'}, dimensions={1} | all-to-all | bytes 2097152 | tf_op jit(solution)/shard_map/all_to_all | solution.py:17
  199.9 0.3 fusion.26
  200.3 0.4 multiply_reduce_fusion
  200.7 0.3 convert_bitcast_fusion
  201.0 0.0 copy-start.6
  201.1 0.2 copy.74
  201.3 0.4 copy-done.6
  201.7 0.3 fusion.17
  202.0 2.5 %fusion.21 = bf16[128,8,512]{2,0,1:T(8,128)(2,1)S(1)} fusion(f32[640,8,512]{2,0,1:T(8,128)} %copy-done.1, bf16[128,8,512]{2,1,0:T(8,128)(2,1)S(1)} %fusion.17, f32[8,512]{1,0:T(8,128)S(1)} %dynamic-slice_convert_fusion, bf16[128,128]{1,0:T(8,128)(2,1)S(1)} %copy-done), kind=kOutput, calls=%fused_computation.35 | convolution fusion | flops 137363456 | bytes 4243456 | tf_op jit(solution)/shard_map/hc,hij->cij/dot_general | solution.py:52
  204.6 0.6 copy.77
  205.1 19.6 %all_to_all.94 = bf16[128,8,512]{2,1,0:T(8,128)(2,1)S(1)} all-to-all(bf16[128,8,512]{2,1,0:T(8,128)(2,1)S(1)} %copy.77), channel_id=1, replica_groups=mesh['gx'=8,'gy'=2,'gz'=16] {'gz'}, dimensions={0} | all-to-all | bytes 2097152 | tf_op jit(solution)/shard_map/all_to_all | solution.py:17
  224.7 1.1 copy.96
  (18 shorter events, 0.1 us)
Async XLA Ops:
  0.0 202.0 %copy-start = (bf16[128,128]{1,0:T(8,128)(2,1)S(1)}, bf16[128,128]{1,0:T(8,128)(2,1)}, u32[]{:S(2)}) copy-start(bf16[128,128]{1,0:T(8,128)(2,1)} %param.13) | copy-start | bytes 98308
  0.0 10.3 %copy-start.3 = (bf16[4,128,128]{2,1,0:T(8,128)(2,1)S(1)}, bf16[4,128,128]{2,1,0:T(8,128)(2,1)}, u32[]{:S(2)}) copy-start(bf16[4,128,128]{2,1,0:T(8,128)(2,1)} %param.10) | copy-start | bytes 393220
  0.0 10.8 %copy-start.4 = (bf16[128,128]{1,0:T(8,128)(2,1)S(1)}, bf16[128,128]{1,0:T(8,128)(2,1)}, u32[]{:S(2)}) copy-start(bf16[128,128]{1,0:T(8,128)(2,1)} %param.11) | copy-start | bytes 98308
  2.8 23.3 %all-to-all-start = ((bf16[8,128,512]{2,0,1:T(8,128)(2,1)}), bf16[8,128,512]{2,0,1:T(8,128)(2,1)S(1)}, u32[]{:S(2)}, u32[]{:S(2)}) async-start(bf16[8,128,512]{2,0,1:T(8,128)(2,1)} %copy.65), calls=%async_computation | async-start | bytes 2097152 | tf_op jit(solution)/shard_map/all_to_all | solution.py:17
  10.3 16.3 %copy-start.5 = (f32[128]{0:T(128)S(1)}, f32[128]{0:T(128)}, u32[]{:S(2)}) copy-start(f32[128]{0:T(128)} %param.9) | copy-start | bytes 1540
  28.2 4.0 %copy-start.1 = (f32[640,8,512]{2,0,1:T(8,128)}, f32[640,8,512]{2,0,1:T(8,128)S(1)}, u32[]{:S(2)}) copy-start(f32[640,8,512]{2,0,1:T(8,128)S(1)} %fusion.23) | copy-start | bytes 31457284
  123.4 1.4 copy-start.2
  201.0 0.7 copy-start.6
